TPU v7x, 32 devices: a whole 2x2x4 slice. The times are simulated.
32 devices in a mesh: gx: 16 (over z, y, core), gy: 2 (over x).
Axes of the slice: x: 2, y: 2, z: 4, core: 2. Of those that a mesh axis runs over, the one named last changes fastest.
Arguments:
- prognostic_values: float32 [3, 6, 2048, 1024], P(None, None, 'gx', 'gy'), may hold values from -6 to 6
- forcing_host_values: bfloat16 [3, 6, 2048, 1024], P(None, None, 'gx', 'gy'), may hold values from -6 to 6
- strength: float32 [3, 6], replicated, may hold values from 50 to 200
- level_height: float32 [3], replicated, may hold values from 0.2 to 3
- pbl_height: float32 [2048, 1024], P('gx', 'gy'), may hold values from 0.2 to 3
Outputs:
- tendency: bfloat16 [3, 6, 2048, 1024], P(None, None, 'gx', 'gy')
- energy: float32 [3, 6], replicated
All inputs are finite; a program needn't handle non-finite values.
Results may differ from a plain program's by a relative error of at most 0.001.
Values sent between devices are 32-bit elements; how exact they have to be, the bound alone decides.
A program may use at most 64 MiB of HBM per device.

v0:
```python
import functools
import math

import jax
import jax.numpy as jnp
from jax import lax
from jax.experimental import pallas as pl
from jax.experimental.pallas import tpu as pltpu
from jax.sharding import PartitionSpec as P

KX = 32
KY = 32
RAMP_DEPTH = 0.25
LANES = 128
SUB = 8
MESH = pl.DeviceIdType.MESH

F32 = jnp.float32
BF16 = jnp.bfloat16

SINE = [(-1.0) ** k * (math.pi / 2) ** (2 * k + 1) / math.factorial(2 * k + 1) for k in range(7)]


def basis(total, place, wave):
    turns = (2.0 * place + 1.0) * wave
    rest = turns - (4.0 * total) * jnp.floor(turns * (1.0 / (4.0 * total)))
    t = (jnp.abs(rest - 2.0 * total) - total) * (1.0 / total)
    t2 = t * t
    poly = jnp.full(t.shape, SINE[-1], F32)
    for c in SINE[-2::-1]:
        poly = poly * t2 + c
    scale = jnp.where(wave == 0.0, math.sqrt(1.0 / total), math.sqrt(2.0 / total))
    return scale * (poly * t)


def iota(shape, dim):
    return lax.broadcasted_iota(jnp.int32, shape, dim)


def split(x):
    hi = x.astype(BF16)
    return hi, (x - hi.astype(F32)).astype(BF16)


def group_masks(rows):
    lane = iota((rows, LANES), 1) // KY
    return [lane == g for g in range(LANES // KY)]


def plan(fields, n_in):
    slots = [range(f, min(f + n_in, fields)) for f in range(0, fields, n_in)]
    return slots, max(len(slots) - 2, 0)


def synthesize(coef, scale, weight_ref, row, col, numbers, variables, put):
    size, cols = coef.shape[0], col.shape[1]
    count = size // SUB
    groups = KX // SUB
    scaled = coef * scale
    stack = jnp.concatenate([jnp.where(m, scaled, 0.0) for m in group_masks(size)], axis=0)
    hi, lo = split(stack)
    lhs = jnp.concatenate([hi, lo, hi], axis=1)
    wave = jnp.dot(lhs, col, preferred_element_type=F32).reshape(groups, count, SUB, cols)
    for k, f in enumerate(numbers):
        whole = jnp.concatenate([wave[g, k] for g in range(groups)], axis=0)
        hi, lo = split(whole)
        rhs = jnp.concatenate([hi, lo, hi, lo], axis=0)
        recon = jnp.dot(row, rhs, preferred_element_type=F32)
        put(k, f, (weight_ref[f // variables] * recon).astype(BF16))


def analysis_kernel(
    dims, prog_hbm, forc_hbm, strength_hbm, level_hbm, pbl_hbm,
    coef_ref, scale_ref, weight_ref, row_ref, col_ref, early_ref,
    strength, level, pbl, prog, forc, part, mine, got_in, total, got_out, full,
    prog_sem, forc_sem, aux_sem, in_send, in_recv, out_send, out_recv, all_send, all_recv,
):
    gx, gy, n_mid, chunk = dims
    fields, rows, cols = prog.shape
    levels, variables = strength.shape
    n_chunks = fields // chunk
    groups = KX // SUB
    n_in, n_out = n_mid * gy, gx // n_mid
    slots, n_early = plan(fields, n_in)
    ix, iy = lax.axis_index("gx"), lax.axis_index("gy")
    outer, mid = ix // n_mid, lax.rem(ix, n_mid)
    me = mid * gy + iy

    def fetch(c):
        span = pl.ds(c * chunk, chunk)
        return (
            pltpu.make_async_copy(prog_hbm.at[span], prog.at[span], prog_sem.at[c]),
            pltpu.make_async_copy(forc_hbm.at[span], forc.at[span], forc_sem.at[c]),
        )

    for c in range(n_chunks):
        for copy in fetch(c):
            copy.start()
    aux = [
        pltpu.make_async_copy(pbl_hbm, pbl, aux_sem.at[0]),
        pltpu.make_async_copy(strength_hbm, strength, aux_sem.at[1]),
        pltpu.make_async_copy(level_hbm, level, aux_sem.at[2]),
    ]
    for copy in aux:
        copy.start()

    def inner_peer(d):
        other = lax.rem(me + d, n_in)
        return other, (outer * n_mid + other // gy, lax.rem(other, gy))

    def outer_peer(d):
        return (lax.rem(outer + d, n_out) * n_mid + mid, iy)

    def where_owned(s, owner, act):
        if len(slots[s]) == n_in:
            act()
        else:
            pl.when(owner < len(slots[s]))(act)

    barrier = pltpu.get_barrier_semaphore()
    for d in range(1, n_in):
        pl.semaphore_signal(barrier, inc=1, device_id=inner_peer(d)[1], device_id_type=MESH)
    for d in range(1, n_out):
        pl.semaphore_signal(barrier, inc=1, device_id=outer_peer(d), device_id_type=MESH)

    row = basis(
        rows * gx,
        (ix * rows + iota((KX, rows), 1)).astype(F32),
        iota((KX, rows), 0).astype(F32),
    )
    row_hi, row_lo = split(row)
    row_lhs = jnp.concatenate([row_hi, row_lo], axis=0)
    row_lhs = jnp.concatenate([row_lhs, row_lhs], axis=1)
    col = basis(
        cols * gy,
        (iy * cols + iota((cols, LANES), 0)).astype(F32),
        lax.rem(iota((cols, LANES), 1), KY).astype(F32),
    )
    col_rhs = jnp.concatenate(split(col), axis=1)

    def one_chunk(c, carry):
        for copy in fetch(c):
            copy.wait()
        for k in range(chunk):
            f = c * chunk + k
            diff = forc[f].astype(F32) - prog[f]
            rhs = jnp.concatenate(split(diff), axis=0)
            both = jnp.dot(row_lhs, rhs, preferred_element_type=F32)
            both = both[:KX] + both[KX:]
            for g in range(groups):
                part[g, f] = both[g * SUB:(g + 1) * SUB]
        return carry

    def to_owner(s, d):
        other, device = inner_peer(d)
        return other, pltpu.make_async_remote_copy(
            src_ref=mine.at[s, other], dst_ref=got_in.at[s, d - 1],
            send_sem=in_send.at[s, d - 1], recv_sem=in_recv.at[s, d - 1],
            device_id=device, device_id_type=MESH,
        )

    def to_plane(s, d):
        return pltpu.make_async_remote_copy(
            src_ref=total.at[s], dst_ref=got_out.at[s, d - 1],
            send_sem=out_send.at[s, d - 1], recv_sem=out_recv.at[s, d - 1],
            device_id=outer_peer(d), device_id_type=MESH,
        )

    def to_all(s, d):
        return pltpu.make_async_remote_copy(
            src_ref=full.at[s, me], dst_ref=full.at[s, me],
            send_sem=all_send.at[s, d - 1], recv_sem=all_recv.at[s, d - 1],
            device_id=inner_peer(d)[1], device_id_type=MESH,
        )

    for s, numbers in enumerate(slots):
        first, count = numbers[0], len(numbers)
        lax.fori_loop(first // chunk, (first + count) // chunk, one_chunk, 0)
        size = count * SUB
        hi, lo = split(part[:, first:first + count].reshape(groups * size, cols))
        both = jnp.dot(hi, col_rhs, preferred_element_type=F32) + jnp.dot(
            lo, col_rhs, preferred_element_type=F32
        )
        both = both[:, :LANES] + both[:, LANES:]
        coef = both[:size]
        for g, mask in list(enumerate(group_masks(size)))[1:]:
            coef = jnp.where(mask, both[g * size:(g + 1) * size], coef)
        for k in range(count):
            mine[s, k] = coef[k * SUB:(k + 1) * SUB]
        if s == 0:
            pl.semaphore_wait(barrier, n_in - 1 + n_out - 1)
        for d in range(1, n_in):
            other, copy = to_owner(s, d)
            where_owned(s, other, copy.start)

    for copy in aux:
        copy.wait()
    for l in range(levels):
        weight_ref[l] = 1.0 / (1.0 + jnp.exp(-(level[l] - pbl[...]) / RAMP_DEPTH))
        for v in range(variables):
            f = l * variables + v
            scale_ref[f * SUB:(f + 1) * SUB] = jnp.full((SUB, LANES), strength[l, v], F32)
    col_hi, col_lo = split(basis(
        cols * gy,
        (iy * cols + iota((LANES, cols), 1)).astype(F32),
        lax.rem(iota((LANES, cols), 0), KY).astype(F32),
    ))
    col_ref[...] = jnp.concatenate([col_hi, col_hi, col_lo], axis=0)
    row_hi, row_lo = split(basis(
        rows * gx,
        (ix * rows + iota((rows, 4 * KX), 0)).astype(F32),
        lax.rem(iota((rows, 4 * KX), 1), KX).astype(F32),
    ))
    row_ref[...] = jnp.where(
        iota((rows, 4 * KX), 1) < 2 * KX, row_hi.astype(F32), row_lo.astype(F32)
    ).astype(BF16)

    for s in range(len(slots)):
        def reduce_in(s=s):
            acc = mine[s, me]
            for d in range(1, n_in):
                to_owner(s, d)[1].wait_recv()
                acc = acc + got_in[s, d - 1]
            total[s] = acc
            for d in range(1, n_out):
                to_plane(s, d).start()
        where_owned(s, me, reduce_in)
    for s in range(len(slots)):
        def reduce_out(s=s):
            acc = total[s]
            for d in range(1, n_out):
                to_plane(s, d).wait_recv()
                acc = acc + got_out[s, d - 1]
            full[s, me] = acc
            for d in range(1, n_in):
                to_all(s, d).start()
        where_owned(s, me, reduce_out)
    for s, numbers in enumerate(slots):
        for d in range(1, n_in):
            sender = lax.rem(me + n_in - d, n_in)
            where_owned(s, sender, to_all(s, d).wait_recv)
        for k, f in enumerate(numbers):
            coef_ref[f * SUB:(f + 1) * SUB] = full[s, k]
        if s < n_early:
            span = slice(numbers[0] * SUB, (numbers[-1] + 1) * SUB)

            def keep(k, f, value):
                early_ref[f] = value

            synthesize(
                coef_ref[span], scale_ref[span], weight_ref, row_ref[...], col_ref[...],
                numbers, variables, keep,
            )
    for s in range(len(slots)):
        for d in range(1, n_in):
            other, copy = to_owner(s, d)
            where_owned(s, other, copy.wait_send)

        def sent(s=s):
            for d in range(1, n_out):
                to_plane(s, d).wait_send()
            for d in range(1, n_in):
                to_all(s, d).wait_send()
        where_owned(s, me, sent)


def synthesis_kernel(
    done, coef_ref, scale_ref, weight_ref, row_ref, col_ref, early_ref, tend_hbm, energy_ref,
    tend, tend_sem,
):
    levels, variables = energy_ref.shape
    fields = levels * variables

    def out(f):
        source = early_ref.at[f] if f < done else tend.at[f - done]
        return pltpu.make_async_copy(
            source, tend_hbm.at[f // variables, f % variables], tend_sem.at[f]
        )

    for f in range(done):
        out(f).start()

    def keep(k, f, value):
        tend[f - done] = value
        if k:
            out(f - 1).start()

    coef = coef_ref[...]
    synthesize(
        coef[done * SUB:], scale_ref[done * SUB:], weight_ref, row_ref[...], col_ref[...],
        range(done, fields), variables, keep,
    )
    out(fields - 1).start()

    power = coef * coef
    at_row = iota((levels, variables), 0)
    at_col = iota((levels, variables), 1)
    energy = jnp.zeros((levels, variables), F32)
    for l in range(levels):
        for v in range(variables):
            f = l * variables + v
            one = jnp.sum(power[f * SUB:(f + 1) * SUB], axis=(0, 1), keepdims=True)
            energy = jnp.where((at_row == l) & (at_col == v), one, energy)
    energy_ref[...] = energy * (1.0 / (KX * KY))

    for f in range(fields):
        out(f).wait()


def per_device(gx, gy, prognostic_values, forcing_host_values, strength, level_height, pbl_height):
    levels, variables, rows, cols = prognostic_values.shape
    fields = levels * variables
    groups = KX // SUB
    n_mid = gx
    n_in, n_out = n_mid * gy, gx // n_mid
    slots, n_early = plan(fields, n_in)
    n_slots = len(slots)
    done = n_early * n_in
    chunk = math.gcd(fields, n_in)
    n_chunks = fields // chunk
    near, far = max(n_in - 1, 1), max(n_out - 1, 1)
    anywhere = pl.BlockSpec(memory_space=pl.ANY)
    vmem = pl.BlockSpec(memory_space=pltpu.VMEM)
    dma = pltpu.SemaphoreType.DMA
    held = pl.pallas_call(
        functools.partial(analysis_kernel, (gx, gy, n_mid, chunk)),
        out_shape=(
            pltpu.VMEM((fields * SUB, LANES), F32),
            pltpu.VMEM((fields * SUB, LANES), F32),
            pltpu.VMEM((levels, rows, cols), F32),
            pltpu.VMEM((rows, 4 * KX), BF16),
            pltpu.VMEM((3 * LANES, cols), BF16),
            pltpu.VMEM((max(done, 1), rows, cols), BF16),
        ),
        in_specs=[anywhere] * 5,
        out_specs=(vmem,) * 6,
        scratch_shapes=[
            pltpu.SMEM((levels, variables), F32),
            pltpu.SMEM((levels,), F32),
            pltpu.VMEM((rows, cols), F32),
            pltpu.VMEM((fields, rows, cols), F32),
            pltpu.VMEM((fields, rows, cols), BF16),
            pltpu.VMEM((groups, fields, SUB, cols), F32),
            pltpu.VMEM((n_slots, n_in, SUB, LANES), F32),
            pltpu.VMEM((n_slots, near, SUB, LANES), F32),
            pltpu.VMEM((n_slots, SUB, LANES), F32),
            pltpu.VMEM((n_slots, far, SUB, LANES), F32),
            pltpu.VMEM((n_slots, n_in, SUB, LANES), F32),
            dma((n_chunks,)),
            dma((n_chunks,)),
            dma((3,)),
            dma((n_slots, near)),
            dma((n_slots, near)),
            dma((n_slots, far)),
            dma((n_slots, far)),
            dma((n_slots, near)),
            dma((n_slots, near)),
        ],
        compiler_params=pltpu.CompilerParams(collective_id=0, has_side_effects=True),
        name="analysis",
    )(
        prognostic_values.reshape(fields, rows, cols),
        forcing_host_values.reshape(fields, rows, cols),
        strength,
        level_height,
        pbl_height,
    )
    tendency, energy = pl.pallas_call(
        functools.partial(synthesis_kernel, done),
        out_shape=(
            jax.ShapeDtypeStruct((levels, variables, rows, cols), BF16),
            jax.ShapeDtypeStruct((levels, variables), F32),
        ),
        in_specs=[vmem] * 6,
        out_specs=(anywhere, vmem),
        scratch_shapes=[
            pltpu.VMEM((fields - done, rows, cols), BF16),
            dma((fields,)),
        ],
        name="synthesis",
    )(*[pltpu.with_memory_space_constraint(x, pltpu.VMEM) for x in held])
    return tendency, energy


def solution(mesh):
    return jax.shard_map(
        functools.partial(per_device, mesh.shape["gx"], mesh.shape["gy"]),
        mesh=mesh,
        in_specs=(P(None, None, "gx", "gy"), P(None, None, "gx", "gy"), P(), P(), P("gx", "gy")),
        out_specs=(P(None, None, "gx", "gy"), P()),
        check_vma=False,
    )
```

profile of v0, /device:TPU:0, one launch (start us, length us, event | category | flops | bytes accessed | tf_op | source)
XLA Modules:
  0.0 20.6 jit_solution(4360658843444845566)
XLA Ops:
  0.6 17.2 %analysis.1 = (f32[144,128]{1,0:T(8,128)S(1)}, f32[144,128]{1,0:T(8,128)S(1)}, f32[3,128,512]{2,1,0:T(8,128)S(1)}, bf16[128,128]{1,0:T(8,128)(2,1)S(1)}, bf16[38...) custom-call(f32[18,128,512]{2,1,0:T(8,128)} %bitcast.2, bf16[18,128,512]{2,1,0:T(8,128)(2,1)} %bitcast.3, ...), custom_call_target="tpu_custom_call" | custom-call | tf_op jit(solution)/shard_map/analysis/pallas_call | solution.py:325
  17.9 2.8 %synthesis.1 = (bf16[3,6,128,512]{3,2,1,0:T(8,128)(2,1)}, f32[3,6]{1,0:T(4,128)}) custom-call(f32[144,128]{1,0:T(8,128)S(1)} %get-tuple-element.8.coef_ref, f32[144,128]{1,0:T(8,128)S(1)} %get-tuple-element.9.scale_ref, f32[3,128,512]{2,1,0:T(8,128)S(1)} %get-tuple-element.10.weight_ref, bf16[128,128]{1,0:T(8,128)(2,1)S(1)} %get-tuple-element.11.row_ref, ...), custom_call_target="tpu_custom_call" | custom-call | tf_op jit(solution)/shard_map/synthesis/pallas_call | solution.py:368
where the time goes:
time: 20.8 us; the launch traced here: 20.6 us
  Pallas kernels  20 us (96%)
  between operations  0.64 us (3%)
    pallas_call x1, Pallas kernels, per_device(): pl.pallas_call(functools.partial(analysis_kernel, (gx, gy, n_mid, chunk))...  17.2 us
    pallas_call x1, Pallas kernels, per_device(): pl.pallas_call(functools.partial(synthesis_kernel, done), out_shape=(jax....  2.78 us

commit v1 on v0

--- a/solution.py
+++ b/solution.py
@@ -14,6 +14,8 @@
 LANES = 128
 SUB = 8
 MESH = pl.DeviceIdType.MESH
+SPLIT = (4, 7)
+FAR = 3
 
 F32 = jnp.float32
 BF16 = jnp.bfloat16
@@ -47,9 +49,26 @@
     return [lane == g for g in range(LANES // KY)]
 
 
-def plan(fields, n_in):
-    slots = [range(f, min(f + n_in, fields)) for f in range(0, fields, n_in)]
-    return slots, max(len(slots) - 2, 0)
+def hops(ix, iy):
+    return ix // 4 + (ix // 2) % 2 + iy
+
+
+def plan_owners(gx, gy, fields):
+    ends = [(ix, iy) for ix in range(gx) for iy in range(gy) if gx % 2 or ix % 2]
+    ends.sort(key=lambda p: hops(*p))
+    ends = ends[:max(1, min(fields, len(ends) - 1))]
+    extra = [ends[1 + i % (len(ends) - 1)] if len(ends) > 1 else ends[0] for i in range(fields - len(ends))]
+    owners = ends[:0:-1] + extra + ends[:1]
+    places = [owners[:f].count(owners[f]) for f in range(fields)]
+    return owners, places
+
+
+def plan_slots(fields):
+    chunk = 2 if fields % 2 == 0 else 1
+    units = fields // chunk
+    cuts = [0, units * SPLIT[0] // 9, units * SPLIT[1] // 9, units]
+    slots = [range(i * chunk, j * chunk) for i, j in zip(cuts, cuts[1:]) if j > i]
+    return slots, chunk
 
 
 def synthesize(coef, scale, weight_ref, row, col, numbers, variables, put):
@@ -72,19 +91,20 @@
 def analysis_kernel(
     dims, prog_hbm, forc_hbm, strength_hbm, level_hbm, pbl_hbm,
     coef_ref, scale_ref, weight_ref, row_ref, col_ref, early_ref,
-    strength, level, pbl, prog, forc, part, mine, got_in, total, got_out, full,
-    prog_sem, forc_sem, aux_sem, in_send, in_recv, out_send, out_recv, all_send, all_recv,
+    strength, level, pbl, prog, forc, part, mine, got, full,
+    prog_sem, forc_sem, aux_sem, part_send, part_recv, full_send, full_recv,
 ):
-    gx, gy, n_mid, chunk = dims
+    gx, gy = dims
     fields, rows, cols = prog.shape
     levels, variables = strength.shape
-    n_chunks = fields // chunk
     groups = KX // SUB
-    n_in, n_out = n_mid * gy, gx // n_mid
-    slots, n_early = plan(fields, n_in)
+    n_dev = gx * gy
+    owners, places = plan_owners(gx, gy, fields)
+    slots, chunk = plan_slots(fields)
+    n_owned = max(places) + 1
     ix, iy = lax.axis_index("gx"), lax.axis_index("gy")
-    outer, mid = ix // n_mid, lax.rem(ix, n_mid)
-    me = mid * gy + iy
+    me = ix * gy + iy
+    far = hops(ix, iy)
 
     def fetch(c):
         span = pl.ds(c * chunk, chunk)
@@ -93,7 +113,7 @@
             pltpu.make_async_copy(forc_hbm.at[span], forc.at[span], forc_sem.at[c]),
         )
 
-    for c in range(n_chunks):
+    for c in range(fields // chunk):
         for copy in fetch(c):
             copy.start()
     aux = [
@@ -104,24 +124,34 @@
     for copy in aux:
         copy.start()
 
-    def inner_peer(d):
-        other = lax.rem(me + d, n_in)
-        return other, (outer * n_mid + other // gy, lax.rem(other, gy))
-
-    def outer_peer(d):
-        return (lax.rem(outer + d, n_out) * n_mid + mid, iy)
-
-    def where_owned(s, owner, act):
-        if len(slots[s]) == n_in:
-            act()
+    def owned(f):
+        return (ix == owners[f][0]) & (iy == owners[f][1])
+
+    owns = [sum(((owned(f)).astype(jnp.int32) for f in range(fields) if places[f] == k), jnp.int32(0)) for k in range(n_owned)]
+    field_at = [
+        sum((owned(f).astype(jnp.int32) * f for f in range(fields) if places[f] == k), jnp.int32(0))
+        for k in range(n_owned)
+    ]
+
+    def each_other(act):
+        def body(j, carry):
+            t = j + (j >= me).astype(jnp.int32)
+            act((t // gy, lax.rem(t, gy)))
+            return carry
+        if n_dev <= 64:
+            for j in range(n_dev - 1):
+                body(j, 0)
         else:
-            pl.when(owner < len(slots[s]))(act)
+            lax.fori_loop(0, n_dev - 1, body, 0)
 
     barrier = pltpu.get_barrier_semaphore()
-    for d in range(1, n_in):
-        pl.semaphore_signal(barrier, inc=1, device_id=inner_peer(d)[1], device_id_type=MESH)
-    for d in range(1, n_out):
-        pl.semaphore_signal(barrier, inc=1, device_id=outer_peer(d), device_id_type=MESH)
+
+    @pl.when(owns[0] > 0)
+    def _():
+        each_other(lambda t: pl.semaphore_signal(barrier, inc=1, device_id=t, device_id_type=MESH))
+
+    def enter():
+        pl.semaphore_wait(barrier, len(set(owners)) - owns[0])
 
     row = basis(
         rows * gx,
@@ -151,28 +181,27 @@
                 part[g, f] = both[g * SUB:(g + 1) * SUB]
         return carry
 
-    def to_owner(s, d):
-        other, device = inner_peer(d)
-        return other, pltpu.make_async_remote_copy(
-            src_ref=mine.at[s, other], dst_ref=got_in.at[s, d - 1],
-            send_sem=in_send.at[s, d - 1], recv_sem=in_recv.at[s, d - 1],
-            device_id=device, device_id_type=MESH,
+    def to_owner(f):
+        ox, oy = owners[f]
+        at = ox * gy + oy
+        return pltpu.make_async_remote_copy(
+            src_ref=mine.at[f], dst_ref=got.at[places[f], me - (me > at).astype(jnp.int32)],
+            send_sem=part_send.at[f], recv_sem=part_recv.at[places[f]],
+            device_id=(ox, oy), device_id_type=MESH,
         )
 
-    def to_plane(s, d):
+    def elsewhere(f, act):
+        pl.when(jnp.logical_not(owned(f)))(act)
+
+    def to_all(k, f, target):
         return pltpu.make_async_remote_copy(
-            src_ref=total.at[s], dst_ref=got_out.at[s, d - 1],
-            send_sem=out_send.at[s, d - 1], recv_sem=out_recv.at[s, d - 1],
-            device_id=outer_peer(d), device_id_type=MESH,
+            src_ref=full.at[f], dst_ref=full.at[f],
+            send_sem=full_send.at[k], recv_sem=full_recv.at[f],
+            device_id=target, device_id_type=MESH,
         )
 
-    def to_all(s, d):
-        return pltpu.make_async_remote_copy(
-            src_ref=full.at[s, me], dst_ref=full.at[s, me],
-            send_sem=all_send.at[s, d - 1], recv_sem=all_recv.at[s, d - 1],
-            device_id=inner_peer(d)[1], device_id_type=MESH,
-        )
-
+    last = len(slots) - 1
+    gate = jnp.where(far >= FAR, 0, jnp.where(far > 0, max(last - 1, 0), last))
     for s, numbers in enumerate(slots):
         first, count = numbers[0], len(numbers)
         lax.fori_loop(first // chunk, (first + count) // chunk, one_chunk, 0)
@@ -185,13 +214,19 @@
         coef = both[:size]
         for g, mask in list(enumerate(group_masks(size)))[1:]:
             coef = jnp.where(mask, both[g * size:(g + 1) * size], coef)
-        for k in range(count):
-            mine[s, k] = coef[k * SUB:(k + 1) * SUB]
-        if s == 0:
-            pl.semaphore_wait(barrier, n_in - 1 + n_out - 1)
-        for d in range(1, n_in):
-            other, copy = to_owner(s, d)
-            where_owned(s, other, copy.start)
+        for k, f in enumerate(numbers):
+            mine[f] = coef[k * SUB:(k + 1) * SUB]
+
+        @pl.when(gate == s)
+        def _(s=s):
+            enter()
+            for f in range(slots[s][0]):
+                elsewhere(f, to_owner(f).start)
+
+        @pl.when(gate <= s)
+        def _(numbers=numbers):
+            for f in numbers:
+                elsewhere(f, to_owner(f).start)
 
     for copy in aux:
         copy.wait()
@@ -215,33 +250,19 @@
         iota((rows, 4 * KX), 1) < 2 * KX, row_hi.astype(F32), row_lo.astype(F32)
     ).astype(BF16)
 
-    for s in range(len(slots)):
-        def reduce_in(s=s):
-            acc = mine[s, me]
-            for d in range(1, n_in):
-                to_owner(s, d)[1].wait_recv()
-                acc = acc + got_in[s, d - 1]
-            total[s] = acc
-            for d in range(1, n_out):
-                to_plane(s, d).start()
-        where_owned(s, me, reduce_in)
-    for s in range(len(slots)):
-        def reduce_out(s=s):
-            acc = total[s]
-            for d in range(1, n_out):
-                to_plane(s, d).wait_recv()
-                acc = acc + got_out[s, d - 1]
-            full[s, me] = acc
-            for d in range(1, n_in):
-                to_all(s, d).start()
-        where_owned(s, me, reduce_out)
+    for k in range(n_owned):
+        @pl.when(owns[k] > 0)
+        def _(k=k):
+            f = field_at[k]
+            pltpu.make_async_copy(got.at[k], got.at[k], part_recv.at[k]).wait()
+            full[f] = mine[f] + jnp.sum(got[k], axis=0)
+            each_other(lambda t: to_all(k, f, t).start())
+
     for s, numbers in enumerate(slots):
-        for d in range(1, n_in):
-            sender = lax.rem(me + n_in - d, n_in)
-            where_owned(s, sender, to_all(s, d).wait_recv)
-        for k, f in enumerate(numbers):
-            coef_ref[f * SUB:(f + 1) * SUB] = full[s, k]
-        if s < n_early:
+        for f in numbers:
+            elsewhere(f, to_all(0, f, owners[f]).wait_recv)
+            coef_ref[f * SUB:(f + 1) * SUB] = full[f]
+        if s < last:
             span = slice(numbers[0] * SUB, (numbers[-1] + 1) * SUB)
 
             def keep(k, f, value):
@@ -251,17 +272,12 @@
                 coef_ref[span], scale_ref[span], weight_ref, row_ref[...], col_ref[...],
                 numbers, variables, keep,
             )
-    for s in range(len(slots)):
-        for d in range(1, n_in):
-            other, copy = to_owner(s, d)
-            where_owned(s, other, copy.wait_send)
-
-        def sent(s=s):
-            for d in range(1, n_out):
-                to_plane(s, d).wait_send()
-            for d in range(1, n_in):
-                to_all(s, d).wait_send()
-        where_owned(s, me, sent)
+    for f in range(fields):
+        elsewhere(f, to_owner(f).wait_send)
+    for k in range(n_owned):
+        @pl.when(owns[k] > 0)
+        def _(k=k):
+            pltpu.make_async_copy(got.at[k], got.at[k], full_send.at[k]).wait()
 
 
 def synthesis_kernel(
@@ -311,19 +327,15 @@
     levels, variables, rows, cols = prognostic_values.shape
     fields = levels * variables
     groups = KX // SUB
-    n_mid = gx
-    n_in, n_out = n_mid * gy, gx // n_mid
-    slots, n_early = plan(fields, n_in)
-    n_slots = len(slots)
-    done = n_early * n_in
-    chunk = math.gcd(fields, n_in)
-    n_chunks = fields // chunk
-    near, far = max(n_in - 1, 1), max(n_out - 1, 1)
+    n_dev = gx * gy
+    slots, chunk = plan_slots(fields)
+    n_owned = max(plan_owners(gx, gy, fields)[1]) + 1
+    done = slots[-1][0]
     anywhere = pl.BlockSpec(memory_space=pl.ANY)
     vmem = pl.BlockSpec(memory_space=pltpu.VMEM)
     dma = pltpu.SemaphoreType.DMA
     held = pl.pallas_call(
-        functools.partial(analysis_kernel, (gx, gy, n_mid, chunk)),
+        functools.partial(analysis_kernel, (gx, gy)),
         out_shape=(
             pltpu.VMEM((fields * SUB, LANES), F32),
             pltpu.VMEM((fields * SUB, LANES), F32),
@@ -341,20 +353,16 @@
             pltpu.VMEM((fields, rows, cols), F32),
             pltpu.VMEM((fields, rows, cols), BF16),
             pltpu.VMEM((groups, fields, SUB, cols), F32),
-            pltpu.VMEM((n_slots, n_in, SUB, LANES), F32),
-            pltpu.VMEM((n_slots, near, SUB, LANES), F32),
-            pltpu.VMEM((n_slots, SUB, LANES), F32),
-            pltpu.VMEM((n_slots, far, SUB, LANES), F32),
-            pltpu.VMEM((n_slots, n_in, SUB, LANES), F32),
-            dma((n_chunks,)),
-            dma((n_chunks,)),
+            pltpu.VMEM((fields, SUB, LANES), F32),
+            pltpu.VMEM((n_owned, n_dev - 1, SUB, LANES), F32),
+            pltpu.VMEM((fields, SUB, LANES), F32),
+            dma((fields // chunk,)),
+            dma((fields // chunk,)),
             dma((3,)),
-            dma((n_slots, near)),
-            dma((n_slots, near)),
-            dma((n_slots, far)),
-            dma((n_slots, far)),
-            dma((n_slots, near)),
-            dma((n_slots, near)),
+            dma((fields,)),
+            dma((n_owned,)),
+            dma((n_owned,)),
+            dma((fields,)),
         ],
         compiler_params=pltpu.CompilerParams(collective_id=0, has_side_effects=True),
         name="analysis",

time: 20.8 us -> 18.7 us (0.90)
  Pallas kernels: 20 us -> 17.9 us
    pallas_call x1, Pallas kernels: 17.2 us -> 15.7 us  [per_device(): pl.pallas_call(functools.partial(analysis_kernel, (gx, gy)), out_shape=(p...]
    pallas_call x1, Pallas kernels: 2.78 us -> 2.26 us  [per_device(): pl.pallas_call(functools.partial(synthesis_kernel, done), out_shape=(jax....]
where the time goes in v1:
time: 18.7 us; the launch traced here: 18.6 us
  Pallas kernels  17.9 us (96%)
  between operations  0.64 us (3%)
    pallas_call x1, Pallas kernels, per_device(): pl.pallas_call(functools.partial(analysis_kernel, (gx, gy)), out_shape=(p...  15.7 us
    pallas_call x1, Pallas kernels, per_device(): pl.pallas_call(functools.partial(synthesis_kernel, done), out_shape=(jax....  2.26 us

profile of v1, /device:TPU:0, one launch (start us, length us, event | category | flops | bytes accessed | tf_op | source)
XLA Modules:
  0.0 18.6 jit_solution(12230543853693885341)
XLA Ops:
  0.6 15.7 %analysis.1 = (f32[144,128]{1,0:T(8,128)S(1)}, f32[144,128]{1,0:T(8,128)S(1)}, f32[3,128,512]{2,1,0:T(8,128)S(1)}, bf16[128,128]{1,0:T(8,128)(2,1)S(1)}, bf16[38...) custom-call(f32[18,128,512]{2,1,0:T(8,128)} %bitcast.2, bf16[18,128,512]{2,1,0:T(8,128)(2,1)} %bitcast.3, ...), custom_call_target="tpu_custom_call" | custom-call | tf_op jit(solution)/shard_map/analysis/pallas_call | solution.py:337
  16.3 2.3 %synthesis.1 = (bf16[3,6,128,512]{3,2,1,0:T(8,128)(2,1)}, f32[3,6]{1,0:T(4,128)}) custom-call(f32[144,128]{1,0:T(8,128)S(1)} %get-tuple-element.8.coef_ref, f32[144,128]{1,0:T(8,128)S(1)} %get-tuple-element.9.scale_ref, f32[3,128,512]{2,1,0:T(8,128)S(1)} %get-tuple-element.10.weight_ref, bf16[128,128]{1,0:T(8,128)(2,1)S(1)} %get-tuple-element.11.row_ref, ...), custom_call_target="tpu_custom_call" | custom-call | tf_op jit(solution)/shard_map/synthesis/pallas_call | solution.py:376

commit v2 on v1

v2 whole, which is shorter than its diff:
```python
import functools
import math

import jax
import jax.numpy as jnp
from jax import lax
from jax.experimental import pallas as pl
from jax.experimental.pallas import tpu as pltpu
from jax.sharding import PartitionSpec as P

KX = 32
KY = 32
RAMP_DEPTH = 0.25
LANES = 128
SUB = 8
MESH = pl.DeviceIdType.MESH
REACH = 3
FAR = 3
TAIL = 1

F32 = jnp.float32
BF16 = jnp.bfloat16

SINE = [(-1.0) ** k * (math.pi / 2) ** (2 * k + 1) / math.factorial(2 * k + 1) for k in range(7)]


def basis(total, place, wave):
    turns = (2.0 * place + 1.0) * wave
    rest = turns - (4.0 * total) * jnp.floor(turns * (1.0 / (4.0 * total)))
    t = (jnp.abs(rest - 2.0 * total) - total) * (1.0 / total)
    t2 = t * t
    poly = jnp.full(t.shape, SINE[-1], F32)
    for c in SINE[-2::-1]:
        poly = poly * t2 + c
    scale = jnp.where(wave == 0.0, math.sqrt(1.0 / total), math.sqrt(2.0 / total))
    return scale * (poly * t)


def iota(shape, dim):
    return lax.broadcasted_iota(jnp.int32, shape, dim)


def split(x):
    hi = x.astype(BF16)
    return hi, (x - hi.astype(F32)).astype(BF16)


def hops(ix, iy):
    return ix // 4 + (ix // 2) % 2 + iy


def plan_groups(fields):
    lanes = LANES // KY
    groups = []
    tile = 0
    for first in range(0, fields, lanes):
        count = min(lanes, fields - first)
        fold = lanes // count
        groups.append((first, count, fold, tile))
        tile += KX // fold // SUB
    return groups, tile


def plan_owners(gx, gy, tiles):
    ends = [(ix, iy) for ix in range(gx) for iy in range(gy) if gx % 2 or ix % 2]
    ends.sort(key=lambda p: hops(*p))
    near = [p for p in ends if hops(*p) <= REACH][:tiles]
    owners = [near[t % len(near)] for t in range(tiles)]
    places = [owners[:t].count(owners[t]) for t in range(tiles)]
    return owners, places


def lane_group(rows):
    return iota((rows, LANES), 1) // KY


def pick(parts, group):
    out = parts[0]
    for i, x in list(enumerate(parts))[1:]:
        out = jnp.where(group == i, x, out)
    return out


def synthesize(coef, count, fold, first, weight_ref, row, col, variables, put):
    group = lane_group(coef.shape[0])
    stack = jnp.concatenate(
        [jnp.where(group == g, coef, 0.0) for g in range(count * fold)], axis=0
    )
    hi, lo = split(stack)
    lhs = jnp.concatenate([hi, lo, hi], axis=1)
    wave = jnp.dot(lhs, col, preferred_element_type=F32)
    for k in range(count):
        f = first + k
        hi, lo = split(wave[k * KX:(k + 1) * KX])
        rhs = jnp.concatenate([hi, lo, hi, lo], axis=0)
        recon = jnp.dot(row, rhs, preferred_element_type=F32)
        put(f, (weight_ref[f // variables] * recon).astype(BF16))


def analysis_kernel(
    dims, prog_hbm, forc_hbm, strength_hbm, level_hbm, pbl_hbm,
    coef_ref, scale_ref, weight_ref, row_ref, col_ref, early_ref,
    strength, level, pbl, prog, forc, part, mine, got, full,
    prog_sem, forc_sem, aux_sem, part_send, part_recv, full_send, full_recv,
):
    gx, gy, tail = dims
    fields, rows, cols = prog.shape
    levels, variables = strength.shape
    n_dev = gx * gy
    groups, tiles = plan_groups(fields)
    owners, places = plan_owners(gx, gy, tiles)
    n_owned = max(places) + 1
    ix, iy = lax.axis_index("gx"), lax.axis_index("gy")
    me = ix * gy + iy
    far = hops(ix, iy)

    def fetch(j):
        first, count = groups[j][:2]
        span = pl.ds(first, count)
        return (
            pltpu.make_async_copy(prog_hbm.at[span], prog.at[span], prog_sem.at[j]),
            pltpu.make_async_copy(forc_hbm.at[span], forc.at[span], forc_sem.at[j]),
        )

    for j in range(len(groups)):
        for copy in fetch(j):
            copy.start()
    aux = [
        pltpu.make_async_copy(pbl_hbm, pbl, aux_sem.at[0]),
        pltpu.make_async_copy(strength_hbm, strength, aux_sem.at[1]),
        pltpu.make_async_copy(level_hbm, level, aux_sem.at[2]),
    ]
    for copy in aux:
        copy.start()

    def owned(t):
        return (ix == owners[t][0]) & (iy == owners[t][1])

    def count_owned(k, weigh):
        return sum(
            (owned(t).astype(jnp.int32) * weigh(t) for t in range(tiles) if places[t] == k),
            jnp.int32(0),
        )

    owns = [count_owned(k, lambda t: 1) for k in range(n_owned)]
    tile_at = [count_owned(k, lambda t: t) for k in range(n_owned)]

    def each_other(act):
        def body(j, carry):
            t = j + (j >= me).astype(jnp.int32)
            act((t // gy, lax.rem(t, gy)))
            return carry
        if n_dev <= 64:
            for j in range(n_dev - 1):
                body(j, 0)
        else:
            lax.fori_loop(0, n_dev - 1, body, 0)

    barrier = pltpu.get_barrier_semaphore()

    @pl.when(owns[0] > 0)
    def _():
        each_other(lambda t: pl.semaphore_signal(barrier, inc=1, device_id=t, device_id_type=MESH))

    def enter():
        pl.semaphore_wait(barrier, len(set(owners)) - owns[0])

    row = basis(
        rows * gx,
        (ix * rows + iota((KX, rows), 1)).astype(F32),
        iota((KX, rows), 0).astype(F32),
    )
    row_hi, row_lo = split(row)
    row_lhs = jnp.concatenate([row_hi, row_lo], axis=0)
    row_lhs = jnp.concatenate([row_lhs, row_lhs], axis=1)
    col = basis(
        cols * gy,
        (iy * cols + iota((cols, LANES), 0)).astype(F32),
        lax.rem(iota((cols, LANES), 1), KY).astype(F32),
    )
    col_rhs = jnp.concatenate(split(col), axis=1)

    def to_owner(t):
        ox, oy = owners[t]
        at = ox * gy + oy
        return pltpu.make_async_remote_copy(
            src_ref=mine.at[t], dst_ref=got.at[places[t], me - (me > at).astype(jnp.int32)],
            send_sem=part_send.at[t], recv_sem=part_recv.at[places[t]],
            device_id=(ox, oy), device_id_type=MESH,
        )

    def elsewhere(t, act):
        pl.when(jnp.logical_not(owned(t)))(act)

    def to_all(k, t, target):
        return pltpu.make_async_remote_copy(
            src_ref=full.at[t], dst_ref=full.at[t],
            send_sem=full_send.at[k], recv_sem=full_recv.at[t],
            device_id=target, device_id_type=MESH,
        )

    def tiles_of(j):
        first, count, fold, tile = groups[j]
        return range(tile, tile + KX // fold // SUB)

    def along_rows(j):
        first, count, fold, tile = groups[j]
        for copy in fetch(j):
            copy.wait()
        for f in range(first, first + count):
            rhs = jnp.concatenate(split(forc[f].astype(F32) - prog[f]), axis=0)
            both = jnp.dot(row_lhs, rhs, preferred_element_type=F32)
            part[f] = both[:KX] + both[KX:]

    def along_cols(j):
        first, count, fold, tile = groups[j]
        hi, lo = split(part[first:first + count].reshape(count * KX, cols))
        both = jnp.dot(hi, col_rhs, preferred_element_type=F32) + jnp.dot(
            lo, col_rhs, preferred_element_type=F32
        )
        both = both[:, :LANES] + both[:, LANES:]
        size = KX // fold
        coef = pick(
            [both[r * size:(r + 1) * size] for r in range(count * fold)], lane_group(size)
        )
        for k, t in enumerate(tiles_of(j)):
            mine[t] = coef[k * SUB:(k + 1) * SUB]

    last = len(groups) - 1
    gate = jnp.where(far >= FAR, 0, jnp.where(far > 0, max(last - 1, 0), last))

    def send(j):
        @pl.when(gate == j)
        def _():
            enter()
            for t in range(tiles_of(j)[0]):
                elsewhere(t, to_owner(t).start)

        @pl.when(gate <= j)
        def _():
            for t in tiles_of(j):
                elsewhere(t, to_owner(t).start)

    for j in range(len(groups)):
        along_rows(j)
        if j:
            along_cols(j - 1)
            send(j - 1)
    along_cols(last)
    send(last)

    for copy in aux:
        copy.wait()
    for l in range(levels):
        weight_ref[l] = 1.0 / (1.0 + jnp.exp(-(level[l] - pbl[...]) / RAMP_DEPTH))
    for j, (first, count, fold, tile) in enumerate(groups):
        scale = pick(
            [
                jnp.full((SUB, LANES), strength[f // variables, f % variables], F32)
                for f in range(first, first + count)
            ],
            lane_group(SUB) // fold,
        )
        for t in tiles_of(j):
            scale_ref[t * SUB:(t + 1) * SUB] = scale
    col_hi, col_lo = split(basis(
        cols * gy,
        (iy * cols + iota((LANES, cols), 1)).astype(F32),
        lax.rem(iota((LANES, cols), 0), KY).astype(F32),
    ))
    col_ref[...] = jnp.concatenate([col_hi, col_hi, col_lo], axis=0)
    row_hi, row_lo = split(basis(
        rows * gx,
        (ix * rows + iota((rows, 4 * KX), 0)).astype(F32),
        lax.rem(iota((rows, 4 * KX), 1), KX).astype(F32),
    ))
    row_ref[...] = jnp.where(
        iota((rows, 4 * KX), 1) < 2 * KX, row_hi.astype(F32), row_lo.astype(F32)
    ).astype(BF16)

    for k in range(n_owned):
        @pl.when(owns[k] > 0)
        def _(k=k):
            t = tile_at[k]
            pltpu.make_async_copy(got.at[k], got.at[k], part_recv.at[k]).wait()
            full[t] = mine[t] + jnp.sum(got[k], axis=0)
            each_other(lambda target: to_all(k, t, target).start())

    for j, (first, count, fold, tile) in enumerate(groups):
        for t in tiles_of(j):
            elsewhere(t, to_all(0, t, owners[t]).wait_recv)
        for t in tiles_of(j):
            coef_ref[t * SUB:(t + 1) * SUB] = full[t]
        if j < len(groups) - tail:
            span = slice(tile * SUB, (tile + len(tiles_of(j))) * SUB)

            def keep(f, value):
                early_ref[f] = value

            synthesize(
                coef_ref[span] * scale_ref[span], count, fold, first,
                weight_ref, row_ref[...], col_ref[...], variables, keep,
            )
    for t in range(tiles):
        elsewhere(t, to_owner(t).wait_send)
    for k in range(n_owned):
        @pl.when(owns[k] > 0)
        def _(k=k):
            pltpu.make_async_copy(got.at[k], got.at[k], full_send.at[k]).wait()


def synthesis_kernel(
    tail, coef_ref, scale_ref, weight_ref, row_ref, col_ref, early_ref, tend_hbm, energy_hbm,
    tend, energy_ref, tend_sem, energy_sem,
):
    levels, variables = energy_ref.shape
    fields = levels * variables
    groups, tiles = plan_groups(fields)
    done = groups[-tail][0]

    def out(f):
        source = early_ref.at[f] if f < done else tend.at[f - done]
        return pltpu.make_async_copy(
            source, tend_hbm.at[f // variables, f % variables], tend_sem.at[f]
        )

    for f in range(done):
        out(f).start()

    def keep(f, value):
        tend[f - done] = value
        if f > done:
            out(f - 1).start()

    for first, count, fold, tile in groups[-tail:]:
        span = slice(tile * SUB, tile * SUB + KX // fold)
        synthesize(
            coef_ref[span] * scale_ref[span], count, fold, first,
            weight_ref, row_ref[...], col_ref[...], variables, keep,
        )
    out(fields - 1).start()

    at_row = iota((levels, variables), 0)
    at_col = iota((levels, variables), 1)
    energy = jnp.zeros((levels, variables), F32)
    for first, count, fold, tile in groups:
        coef = coef_ref[tile * SUB:tile * SUB + KX // fold]
        power = jnp.sum(coef * coef, axis=0, keepdims=True)
        group = lane_group(1) // fold
        for k in range(count):
            f = first + k
            one = jnp.sum(jnp.where(group == k, power, 0.0), axis=(0, 1), keepdims=True)
            energy = jnp.where(
                (at_row == f // variables) & (at_col == f % variables), one, energy
            )
    energy_ref[...] = energy * (1.0 / (KX * KY))
    result = pltpu.make_async_copy(energy_ref, energy_hbm, energy_sem)
    result.start()

    for f in range(fields):
        out(f).wait()
    result.wait()


def per_device(gx, gy, prognostic_values, forcing_host_values, strength, level_height, pbl_height):
    levels, variables, rows, cols = prognostic_values.shape
    fields = levels * variables
    n_dev = gx * gy
    groups, tiles = plan_groups(fields)
    n_owned = max(plan_owners(gx, gy, tiles)[1]) + 1
    tail = min(TAIL, len(groups))
    done = groups[-tail][0]
    anywhere = pl.BlockSpec(memory_space=pl.ANY)
    vmem = pl.BlockSpec(memory_space=pltpu.VMEM)
    dma = pltpu.SemaphoreType.DMA
    held = pl.pallas_call(
        functools.partial(analysis_kernel, (gx, gy, tail)),
        out_shape=(
            pltpu.VMEM((tiles * SUB, LANES), F32),
            pltpu.VMEM((tiles * SUB, LANES), F32),
            pltpu.VMEM((levels, rows, cols), F32),
            pltpu.VMEM((rows, 4 * KX), BF16),
            pltpu.VMEM((3 * LANES, cols), BF16),
            pltpu.VMEM((max(done, 1), rows, cols), BF16),
        ),
        in_specs=[anywhere] * 5,
        out_specs=(vmem,) * 6,
        scratch_shapes=[
            pltpu.SMEM((levels, variables), F32),
            pltpu.SMEM((levels,), F32),
            pltpu.VMEM((rows, cols), F32),
            pltpu.VMEM((fields, rows, cols), F32),
            pltpu.VMEM((fields, rows, cols), BF16),
            pltpu.VMEM((fields, KX, cols), F32),
            pltpu.VMEM((tiles, SUB, LANES), F32),
            pltpu.VMEM((n_owned, n_dev - 1, SUB, LANES), F32),
            pltpu.VMEM((tiles, SUB, LANES), F32),
            dma((len(groups),)),
            dma((len(groups),)),
            dma((3,)),
            dma((tiles,)),
            dma((n_owned,)),
            dma((n_owned,)),
            dma((tiles,)),
        ],
        compiler_params=pltpu.CompilerParams(collective_id=0, has_side_effects=True),
        name="analysis",
    )(
        prognostic_values.reshape(fields, rows, cols),
        forcing_host_values.reshape(fields, rows, cols),
        strength,
        level_height,
        pbl_height,
    )
    tendency, energy = pl.pallas_call(
        functools.partial(synthesis_kernel, tail),
        out_shape=(
            jax.ShapeDtypeStruct((levels, variables, rows, cols), BF16),
            jax.ShapeDtypeStruct((levels, variables), F32),
        ),
        in_specs=[vmem] * 6,
        out_specs=(anywhere, anywhere),
        scratch_shapes=[
            pltpu.VMEM((fields - done, rows, cols), BF16),
            pltpu.VMEM((levels, variables), F32),
            dma((fields,)),
            dma,
        ],
        name="synthesis",
    )(*[pltpu.with_memory_space_constraint(x, pltpu.VMEM) for x in held])
    return tendency, energy


def solution(mesh):
    return jax.shard_map(
        functools.partial(per_device, mesh.shape["gx"], mesh.shape["gy"]),
        mesh=mesh,
        in_specs=(P(None, None, "gx", "gy"), P(None, None, "gx", "gy"), P(), P(), P("gx", "gy")),
        out_specs=(P(None, None, "gx", "gy"), P()),
        check_vma=False,
    )
```

time: 18.7 us -> 17.7 us (0.947)
  Pallas kernels: 17.9 us -> 16.9 us
    pallas_call x2, Pallas kernels: 17.9 us -> 16.9 us  [the longest x1 15.1 us: per_device(): pl.pallas_call(functools.partial(analysis_kernel, (gx, gy, tail)), out_sh...]
where the time goes in v2:
time: 17.7 us; the launch traced here: 17.5 us
  Pallas kernels  16.9 us (95%)
  between operations  0.64 us (4%)
    pallas_call x1, Pallas kernels, per_device(): pl.pallas_call(functools.partial(analysis_kernel, (gx, gy, tail)), out_sh...  15.1 us
    pallas_call x1, Pallas kernels, per_device(): pl.pallas_call(functools.partial(synthesis_kernel, tail), out_shape=(jax....  1.79 us

profile of v2, /device:TPU:0, one launch (start us, length us, event | category | flops | bytes accessed | tf_op | source)
XLA Modules:
  0.0 17.5 jit_solution(2636551480159636182)
XLA Ops:
  0.6 15.1 %analysis.1 = (f32[144,128]{1,0:T(8,128)S(1)}, f32[144,128]{1,0:T(8,128)S(1)}, f32[3,128,512]{2,1,0:T(8,128)S(1)}, bf16[128,128]{1,0:T(8,128)(2,1)S(1)}, bf16[38...) custom-call(f32[18,128,512]{2,1,0:T(8,128)} %bitcast.2, bf16[18,128,512]{2,1,0:T(8,128)(2,1)} %bitcast.3, ...), custom_call_target="tpu_custom_call" | custom-call | tf_op jit(solution)/shard_map/analysis/pallas_call | solution.py:376
  15.7 1.8 %synthesis.1 = (bf16[3,6,128,512]{3,2,1,0:T(8,128)(2,1)}, f32[3,6]{1,0:T(4,128)}) custom-call(f32[144,128]{1,0:T(8,128)S(1)} %get-tuple-element.8.coef_ref, f32[144,128]{1,0:T(8,128)S(1)} %get-tuple-element.9.scale_ref, f32[3,128,512]{2,1,0:T(8,128)S(1)} %get-tuple-element.10.weight_ref, bf16[128,128]{1,0:T(8,128)(2,1)S(1)} %get-tuple-element.11.row_ref, ...), custom_call_target="tpu_custom_call" | custom-call | tf_op jit(solution)/shard_map/synthesis/pallas_call | solution.py:415

commit v3 on v2

--- a/solution.py
+++ b/solution.py
@@ -16,7 +16,7 @@
 MESH = pl.DeviceIdType.MESH
 REACH = 3
 FAR = 3
-TAIL = 1
+TAIL = 2
 
 F32 = jnp.float32
 BF16 = jnp.bfloat16
@@ -81,26 +81,25 @@
     return out
 
 
-def synthesize(coef, count, fold, first, weight_ref, row, col, variables, put):
-    group = lane_group(coef.shape[0])
-    stack = jnp.concatenate(
-        [jnp.where(group == g, coef, 0.0) for g in range(count * fold)], axis=0
-    )
-    hi, lo = split(stack)
+def expand_cols(parts, col):
+    stack = []
+    for coef, count, fold in parts:
+        group = lane_group(coef.shape[0])
+        stack.extend(jnp.where(group == g, coef, 0.0) for g in range(count * fold))
+    hi, lo = split(jnp.concatenate(stack, axis=0))
     lhs = jnp.concatenate([hi, lo, hi], axis=1)
-    wave = jnp.dot(lhs, col, preferred_element_type=F32)
-    for k in range(count):
-        f = first + k
-        hi, lo = split(wave[k * KX:(k + 1) * KX])
-        rhs = jnp.concatenate([hi, lo, hi, lo], axis=0)
-        recon = jnp.dot(row, rhs, preferred_element_type=F32)
-        put(f, (weight_ref[f // variables] * recon).astype(BF16))
+    return split(jnp.dot(lhs, col, preferred_element_type=F32))
+
+
+def expand_rows(hi, lo, row, weight):
+    rhs = jnp.concatenate([hi, lo, hi, lo], axis=0)
+    return (weight * jnp.dot(row, rhs, preferred_element_type=F32)).astype(BF16)
 
 
 def analysis_kernel(
     dims, prog_hbm, forc_hbm, strength_hbm, level_hbm, pbl_hbm,
     coef_ref, scale_ref, weight_ref, row_ref, col_ref, early_ref,
-    strength, level, pbl, prog, forc, part, mine, got, full,
+    strength, level, pbl, prog, forc, part, mine, got, full, wave,
     prog_sem, forc_sem, aux_sem, part_send, part_recv, full_send, full_recv,
 ):
     gx, gy, tail = dims
@@ -133,6 +132,10 @@
     for copy in aux:
         copy.start()
 
+    def tiles_of(j):
+        first, count, fold, tile = groups[j]
+        return range(tile, tile + KX // fold // SUB)
+
     def owned(t):
         return (ix == owners[t][0]) & (iy == owners[t][1])
 
@@ -142,8 +145,17 @@
             jnp.int32(0),
         )
 
+    group_of = [j for j in range(len(groups)) for t in tiles_of(j)]
     owns = [count_owned(k, lambda t: 1) for k in range(n_owned)]
     tile_at = [count_owned(k, lambda t: t) for k in range(n_owned)]
+    group_at = [count_owned(k, lambda t: group_of[t]) for k in range(n_owned)]
+
+    def settle(ref, sem):
+        pltpu.make_async_copy(ref, ref, sem).wait()
+
+    def settle_tiles(buf, sem, first, count, own, most):
+        for c in range(min(most, count - 1) + 1):
+            pl.when(own == c)(lambda c=c: settle(buf.at[pl.ds(first, count - c)], sem))
 
     def each_other(act):
         def body(j, carry):
@@ -185,23 +197,19 @@
         at = ox * gy + oy
         return pltpu.make_async_remote_copy(
             src_ref=mine.at[t], dst_ref=got.at[places[t], me - (me > at).astype(jnp.int32)],
-            send_sem=part_send.at[t], recv_sem=part_recv.at[places[t]],
+            send_sem=part_send, recv_sem=part_recv.at[places[t]],
             device_id=(ox, oy), device_id_type=MESH,
         )
 
     def elsewhere(t, act):
         pl.when(jnp.logical_not(owned(t)))(act)
 
-    def to_all(k, t, target):
+    def to_all(tile, group, target):
         return pltpu.make_async_remote_copy(
-            src_ref=full.at[t], dst_ref=full.at[t],
-            send_sem=full_send.at[k], recv_sem=full_recv.at[t],
+            src_ref=full.at[tile], dst_ref=full.at[tile],
+            send_sem=full_send, recv_sem=full_recv.at[group],
             device_id=target, device_id_type=MESH,
         )
-
-    def tiles_of(j):
-        first, count, fold, tile = groups[j]
-        return range(tile, tile + KX // fold // SUB)
 
     def along_rows(j):
         first, count, fold, tile = groups[j]
@@ -282,31 +290,46 @@
         @pl.when(owns[k] > 0)
         def _(k=k):
             t = tile_at[k]
-            pltpu.make_async_copy(got.at[k], got.at[k], part_recv.at[k]).wait()
+            settle(got.at[k], part_recv.at[k])
             full[t] = mine[t] + jnp.sum(got[k], axis=0)
-            each_other(lambda target: to_all(k, t, target).start())
+            each_other(lambda target: to_all(t, group_at[k], target).start())
+
+    early = len(groups) - tail
+
+    def widen(j):
+        first, count, fold, tile = groups[j]
+        span = slice(tile * SUB, tile * SUB + KX // fold)
+        hi, lo = expand_cols([(coef_ref[span] * scale_ref[span], count, fold)], col_ref[...])
+        wave[j % 2, 0, :count * KX] = hi
+        wave[j % 2, 1, :count * KX] = lo
+
+    def finish(j):
+        first, count, fold, tile = groups[j]
+        for k in range(count):
+            f = first + k
+            span = slice(k * KX, (k + 1) * KX)
+            early_ref[f] = expand_rows(
+                wave[j % 2, 0, span], wave[j % 2, 1, span], row_ref[...],
+                weight_ref[f // variables],
+            )
 
     for j, (first, count, fold, tile) in enumerate(groups):
-        for t in tiles_of(j):
-            elsewhere(t, to_all(0, t, owners[t]).wait_recv)
+        if j == early and j:
+            finish(j - 1)
+        mine_here = sum((owned(t).astype(jnp.int32) for t in tiles_of(j)), jnp.int32(0))
+        held = [owners[t] for t in tiles_of(j)]
+        settle_tiles(
+            full, full_recv.at[j], tile, len(held), mine_here, max(held.count(o) for o in held)
+        )
         for t in tiles_of(j):
             coef_ref[t * SUB:(t + 1) * SUB] = full[t]
-        if j < len(groups) - tail:
-            span = slice(tile * SUB, (tile + len(tiles_of(j))) * SUB)
-
-            def keep(f, value):
-                early_ref[f] = value
-
-            synthesize(
-                coef_ref[span] * scale_ref[span], count, fold, first,
-                weight_ref, row_ref[...], col_ref[...], variables, keep,
-            )
-    for t in range(tiles):
-        elsewhere(t, to_owner(t).wait_send)
-    for k in range(n_owned):
-        @pl.when(owns[k] > 0)
-        def _(k=k):
-            pltpu.make_async_copy(got.at[k], got.at[k], full_send.at[k]).wait()
+        if j < early:
+            widen(j)
+            if j:
+                finish(j - 1)
+    settle_tiles(mine, part_send, 0, tiles, sum(owns), n_owned)
+    for c in range(1, n_owned + 1):
+        pl.when(sum(owns) == c)(lambda c=c: settle(got.at[pl.ds(0, c)], full_send))
 
 
 def synthesis_kernel(
@@ -321,24 +344,11 @@
     def out(f):
         source = early_ref.at[f] if f < done else tend.at[f - done]
         return pltpu.make_async_copy(
-            source, tend_hbm.at[f // variables, f % variables], tend_sem.at[f]
+            source, tend_hbm.at[f // variables, f % variables], tend_sem
         )
 
     for f in range(done):
         out(f).start()
-
-    def keep(f, value):
-        tend[f - done] = value
-        if f > done:
-            out(f - 1).start()
-
-    for first, count, fold, tile in groups[-tail:]:
-        span = slice(tile * SUB, tile * SUB + KX // fold)
-        synthesize(
-            coef_ref[span] * scale_ref[span], count, fold, first,
-            weight_ref, row_ref[...], col_ref[...], variables, keep,
-        )
-    out(fields - 1).start()
 
     at_row = iota((levels, variables), 0)
     at_col = iota((levels, variables), 1)
@@ -357,8 +367,21 @@
     result = pltpu.make_async_copy(energy_ref, energy_hbm, energy_sem)
     result.start()
 
-    for f in range(fields):
-        out(f).wait()
+    parts = []
+    for first, count, fold, tile in groups[-tail:]:
+        span = slice(tile * SUB, tile * SUB + KX // fold)
+        parts.append((coef_ref[span] * scale_ref[span], count, fold))
+    hi, lo = expand_cols(parts, col_ref[...])
+    for f in range(done, fields):
+        span = slice((f - done) * KX, (f - done + 1) * KX)
+        tend[f - done] = expand_rows(
+            hi[span], lo[span], row_ref[...], weight_ref[f // variables]
+        )
+        if f > done:
+            out(f - 1).start()
+    out(fields - 1).start()
+
+    pltpu.make_async_copy(tend_hbm, tend_hbm, tend_sem).wait()
     result.wait()
 
 
@@ -395,13 +418,14 @@
             pltpu.VMEM((tiles, SUB, LANES), F32),
             pltpu.VMEM((n_owned, n_dev - 1, SUB, LANES), F32),
             pltpu.VMEM((tiles, SUB, LANES), F32),
+            pltpu.VMEM((2, 2, LANES, cols), BF16),
             dma((len(groups),)),
             dma((len(groups),)),
             dma((3,)),
-            dma((tiles,)),
+            dma,
             dma((n_owned,)),
-            dma((n_owned,)),
-            dma((tiles,)),
+            dma,
+            dma((len(groups),)),
         ],
         compiler_params=pltpu.CompilerParams(collective_id=0, has_side_effects=True),
         name="analysis",
@@ -423,7 +447,7 @@
         scratch_shapes=[
             pltpu.VMEM((fields - done, rows, cols), BF16),
             pltpu.VMEM((levels, variables), F32),
-            dma((fields,)),
+            dma,
             dma,
         ],
         name="synthesis",

time: 17.7 us -> 16.6 us (0.938)
  Pallas kernels: 16.9 us -> 15.8 us
    pallas_call x1, Pallas kernels: 15.1 us -> 14.3 us  [per_device(): pl.pallas_call(functools.partial(analysis_kernel, (gx, gy, tail)), out_sh...]
    pallas_call x1, Pallas kernels: 1.79 us -> 1.6 us  [per_device(): pl.pallas_call(functools.partial(synthesis_kernel, tail), out_shape=(jax....]
where the time goes in v3:
time: 16.6 us; the launch traced here: 16.5 us
  Pallas kernels  15.8 us (95%)
  between operations  0.64 us (4%)
    pallas_call x1, Pallas kernels, per_device(): pl.pallas_call(functools.partial(analysis_kernel, (gx, gy, tail)), out_sh...  14.3 us
    pallas_call x1, Pallas kernels, per_device(): pl.pallas_call(functools.partial(synthesis_kernel, tail), out_shape=(jax....  1.6 us

profile of v3, /device:TPU:0, one launch (start us, length us, event | category | flops | bytes accessed | tf_op | source)
XLA Modules:
  0.0 16.5 jit_solution(3194721240804307725)
XLA Ops:
  0.6 14.3 %analysis.1 = (f32[144,128]{1,0:T(8,128)S(1)}, f32[144,128]{1,0:T(8,128)S(1)}, f32[3,128,512]{2,1,0:T(8,128)S(1)}, bf16[128,128]{1,0:T(8,128)(2,1)S(1)}, bf16[38...) custom-call(f32[18,128,512]{2,1,0:T(8,128)} %bitcast.2, bf16[18,128,512]{2,1,0:T(8,128)(2,1)} %bitcast.3, ...), custom_call_target="tpu_custom_call" | custom-call | tf_op jit(solution)/shard_map/analysis/pallas_call | solution.py:399
  14.9 1.6 %synthesis.1 = (bf16[3,6,128,512]{3,2,1,0:T(8,128)(2,1)}, f32[3,6]{1,0:T(4,128)}) custom-call(f32[144,128]{1,0:T(8,128)S(1)} %get-tuple-element.8.coef_ref, f32[144,128]{1,0:T(8,128)S(1)} %get-tuple-element.9.scale_ref, f32[3,128,512]{2,1,0:T(8,128)S(1)} %get-tuple-element.10.weight_ref, bf16[128,128]{1,0:T(8,128)(2,1)S(1)} %get-tuple-element.11.row_ref, ...), custom_call_target="tpu_custom_call" | custom-call | tf_op jit(solution)/shard_map/synthesis/pallas_call | solution.py:439

commit v4 on v3

--- a/solution.py
+++ b/solution.py
@@ -17,6 +17,7 @@
 REACH = 3
 FAR = 3
 TAIL = 2
+BLOCK = 4
 
 F32 = jnp.float32
 BF16 = jnp.bfloat16
@@ -61,6 +62,10 @@
     return groups, tile
 
 
+def plan_blocks(fields):
+    return [range(f, min(f + BLOCK, fields)) for f in range(0, fields, BLOCK)]
+
+
 def plan_owners(gx, gy, tiles):
     ends = [(ix, iy) for ix in range(gx) for iy in range(gy) if gx % 2 or ix % 2]
     ends.sort(key=lambda p: hops(*p))
@@ -100,7 +105,7 @@
     dims, prog_hbm, forc_hbm, strength_hbm, level_hbm, pbl_hbm,
     coef_ref, scale_ref, weight_ref, row_ref, col_ref, early_ref,
     strength, level, pbl, prog, forc, part, mine, got, full, wave,
-    prog_sem, forc_sem, aux_sem, part_send, part_recv, full_send, full_recv,
+    load_sem, aux_sem, part_send, part_recv, full_send, full_recv,
 ):
     gx, gy, tail = dims
     fields, rows, cols = prog.shape
@@ -113,16 +118,29 @@
     me = ix * gy + iy
     far = hops(ix, iy)
 
-    def fetch(j):
-        first, count = groups[j][:2]
-        span = pl.ds(first, count)
+    def settle(ref, sem):
+        pltpu.make_async_copy(ref, ref, sem).wait()
+
+    blocks = plan_blocks(fields)
+
+    def fetch(b):
+        span = pl.ds(blocks[b][0], len(blocks[b]))
+        odd = len(blocks[b]) % 2
         return (
-            pltpu.make_async_copy(prog_hbm.at[span], prog.at[span], prog_sem.at[j]),
-            pltpu.make_async_copy(forc_hbm.at[span], forc.at[span], forc_sem.at[j]),
-        )
-
-    for j in range(len(groups)):
-        for copy in fetch(j):
+            pltpu.make_async_copy(prog_hbm.at[span], prog.at[span], load_sem.at[b, 0]),
+            pltpu.make_async_copy(forc_hbm.at[span], forc.at[span], load_sem.at[b, odd]),
+        )
+
+    def loaded(b):
+        count = len(blocks[b])
+        if count % 2:
+            for copy in fetch(b):
+                copy.wait()
+        else:
+            settle(prog.at[pl.ds(0, count + count // 2)], load_sem.at[b, 0])
+
+    for b in range(len(blocks)):
+        for copy in fetch(b):
             copy.start()
     aux = [
         pltpu.make_async_copy(pbl_hbm, pbl, aux_sem.at[0]),
@@ -145,13 +163,11 @@
             jnp.int32(0),
         )
 
-    group_of = [j for j in range(len(groups)) for t in tiles_of(j)]
+    early = len(groups) - tail
+    group_of = [min(j, early) for j in range(len(groups)) for t in tiles_of(j)]
     owns = [count_owned(k, lambda t: 1) for k in range(n_owned)]
     tile_at = [count_owned(k, lambda t: t) for k in range(n_owned)]
     group_at = [count_owned(k, lambda t: group_of[t]) for k in range(n_owned)]
-
-    def settle(ref, sem):
-        pltpu.make_async_copy(ref, ref, sem).wait()
 
     def settle_tiles(buf, sem, first, count, own, most):
         for c in range(min(most, count - 1) + 1):
@@ -211,11 +227,9 @@
             device_id=target, device_id_type=MESH,
         )
 
-    def along_rows(j):
-        first, count, fold, tile = groups[j]
-        for copy in fetch(j):
-            copy.wait()
-        for f in range(first, first + count):
+    def along_rows(b):
+        loaded(b)
+        for f in blocks[b]:
             rhs = jnp.concatenate(split(forc[f].astype(F32) - prog[f]), axis=0)
             both = jnp.dot(row_lhs, rhs, preferred_element_type=F32)
             part[f] = both[:KX] + both[KX:]
@@ -249,11 +263,13 @@
             for t in tiles_of(j):
                 elsewhere(t, to_owner(t).start)
 
-    for j in range(len(groups)):
-        along_rows(j)
-        if j:
-            along_cols(j - 1)
-            send(j - 1)
+    ready = 0
+    for b in range(len(blocks)):
+        along_rows(b)
+        if ready < last and blocks[b][0] >= sum(groups[ready][:2]):
+            along_cols(ready)
+            send(ready)
+            ready += 1
     along_cols(last)
     send(last)
 
@@ -294,8 +310,6 @@
             full[t] = mine[t] + jnp.sum(got[k], axis=0)
             each_other(lambda target: to_all(t, group_at[k], target).start())
 
-    early = len(groups) - tail
-
     def widen(j):
         first, count, fold, tile = groups[j]
         span = slice(tile * SUB, tile * SUB + KX // fold)
@@ -313,20 +327,24 @@
                 weight_ref[f // variables],
             )
 
-    for j, (first, count, fold, tile) in enumerate(groups):
-        if j == early and j:
+    def arrive(stage):
+        here = [t for t in range(tiles) if group_of[t] == stage]
+        held = [owners[t] for t in here]
+        own = sum((owned(t).astype(jnp.int32) for t in here), jnp.int32(0))
+        settle_tiles(
+            full, full_recv.at[stage], here[0], len(here), own, max(held.count(o) for o in held)
+        )
+        for t in here:
+            coef_ref[t * SUB:(t + 1) * SUB] = full[t]
+
+    for j in range(early):
+        arrive(j)
+        widen(j)
+        if j:
             finish(j - 1)
-        mine_here = sum((owned(t).astype(jnp.int32) for t in tiles_of(j)), jnp.int32(0))
-        held = [owners[t] for t in tiles_of(j)]
-        settle_tiles(
-            full, full_recv.at[j], tile, len(held), mine_here, max(held.count(o) for o in held)
-        )
-        for t in tiles_of(j):
-            coef_ref[t * SUB:(t + 1) * SUB] = full[t]
-        if j < early:
-            widen(j)
-            if j:
-                finish(j - 1)
+    if early:
+        finish(early - 1)
+    arrive(early)
     settle_tiles(mine, part_send, 0, tiles, sum(owns), n_owned)
     for c in range(1, n_owned + 1):
         pl.when(sum(owns) == c)(lambda c=c: settle(got.at[pl.ds(0, c)], full_send))
@@ -341,14 +359,17 @@
     groups, tiles = plan_groups(fields)
     done = groups[-tail][0]
 
-    def out(f):
-        source = early_ref.at[f] if f < done else tend.at[f - done]
+    def out(first, count):
+        level, at = first // variables, first % variables
+        span = pl.ds(first - done, count) if first >= done else pl.ds(first, count)
         return pltpu.make_async_copy(
-            source, tend_hbm.at[f // variables, f % variables], tend_sem
-        )
-
-    for f in range(done):
-        out(f).start()
+            (tend if first >= done else early_ref).at[span],
+            tend_hbm.at[level, pl.ds(at, count)],
+            tend_sem,
+        )
+
+    for first in range(0, done, variables):
+        out(first, min(variables, done - first)).start()
 
     at_row = iota((levels, variables), 0)
     at_col = iota((levels, variables), 1)
@@ -378,8 +399,8 @@
             hi[span], lo[span], row_ref[...], weight_ref[f // variables]
         )
         if f > done:
-            out(f - 1).start()
-    out(fields - 1).start()
+            out(f - 1, 1).start()
+    out(fields - 1, 1).start()
 
     pltpu.make_async_copy(tend_hbm, tend_hbm, tend_sem).wait()
     result.wait()
@@ -392,6 +413,7 @@
     groups, tiles = plan_groups(fields)
     n_owned = max(plan_owners(gx, gy, tiles)[1]) + 1
     tail = min(TAIL, len(groups))
+    blocks = plan_blocks(fields)
     done = groups[-tail][0]
     anywhere = pl.BlockSpec(memory_space=pl.ANY)
     vmem = pl.BlockSpec(memory_space=pltpu.VMEM)
@@ -419,13 +441,12 @@
             pltpu.VMEM((n_owned, n_dev - 1, SUB, LANES), F32),
             pltpu.VMEM((tiles, SUB, LANES), F32),
             pltpu.VMEM((2, 2, LANES, cols), BF16),
-            dma((len(groups),)),
-            dma((len(groups),)),
+            dma((len(blocks), 1 + max(len(b) % 2 for b in blocks))),
             dma((3,)),
             dma,
             dma((n_owned,)),
             dma,
-            dma((len(groups),)),
+            dma((len(groups) - tail + 1,)),
         ],
         compiler_params=pltpu.CompilerParams(collective_id=0, has_side_effects=True),
         name="analysis",

time: 16.6 us -> 16.4 us (0.988)
  Pallas kernels: 15.8 us -> 15.6 us
    pallas_call x1, Pallas kernels: 1.6 us -> 1.42 us  [per_device(): pl.pallas_call(functools.partial(synthesis_kernel, tail), out_shape=(jax....]
where the time goes in v4:
time: 16.4 us; the launch traced here: 16.2 us
  Pallas kernels  15.6 us (95%)
  between operations  0.64 us (4%)
    pallas_call x1, Pallas kernels, per_device(): pl.pallas_call(functools.partial(analysis_kernel, (gx, gy, tail)), out_sh...  14.1 us
    pallas_call x1, Pallas kernels, per_device(): pl.pallas_call(functools.partial(synthesis_kernel, tail), out_shape=(jax....  1.42 us

profile of v4, /device:TPU:0, one launch (start us, length us, event | category | flops | bytes accessed | tf_op | source)
XLA Modules:
  0.0 16.2 jit_solution(16376827216903250044)
XLA Ops:
  0.6 14.1 %analysis.1 = (f32[144,128]{1,0:T(8,128)S(1)}, f32[144,128]{1,0:T(8,128)S(1)}, f32[3,128,512]{2,1,0:T(8,128)S(1)}, bf16[128,128]{1,0:T(8,128)(2,1)S(1)}, bf16[38...) custom-call(f32[18,128,512]{2,1,0:T(8,128)} %bitcast.2, bf16[18,128,512]{2,1,0:T(8,128)(2,1)} %bitcast.3, ...), custom_call_target="tpu_custom_call" | custom-call | tf_op jit(solution)/shard_map/analysis/pallas_call | solution.py:421
  14.8 1.4 %synthesis.1 = (bf16[3,6,128,512]{3,2,1,0:T(8,128)(2,1)}, f32[3,6]{1,0:T(4,128)}) custom-call(f32[144,128]{1,0:T(8,128)S(1)} %get-tuple-element.8.coef_ref, f32[144,128]{1,0:T(8,128)S(1)} %get-tuple-element.9.scale_ref, f32[3,128,512]{2,1,0:T(8,128)S(1)} %get-tuple-element.10.weight_ref, bf16[128,128]{1,0:T(8,128)(2,1)S(1)} %get-tuple-element.11.row_ref, ...), custom_call_target="tpu_custom_call" | custom-call | tf_op jit(solution)/shard_map/synthesis/pallas_call | solution.py:460

commit v5 on v4

--- a/solution.py
+++ b/solution.py
@@ -103,9 +103,9 @@
 
 def analysis_kernel(
     dims, prog_hbm, forc_hbm, strength_hbm, level_hbm, pbl_hbm,
-    coef_ref, scale_ref, weight_ref, row_ref, col_ref, early_ref,
+    coef_ref, scale_ref, weight_ref, row_ref, col_ref, early_ref, wide_ref,
     strength, level, pbl, prog, forc, part, mine, got, full, wave,
-    load_sem, aux_sem, part_send, part_recv, full_send, full_recv,
+    load_sem, part_send, part_recv, full_send, full_recv,
 ):
     gx, gy, tail = dims
     fields, rows, cols = prog.shape
@@ -143,11 +143,12 @@
         for copy in fetch(b):
             copy.start()
     aux = [
-        pltpu.make_async_copy(pbl_hbm, pbl, aux_sem.at[0]),
-        pltpu.make_async_copy(strength_hbm, strength, aux_sem.at[1]),
-        pltpu.make_async_copy(level_hbm, level, aux_sem.at[2]),
+        pltpu.make_async_copy(source, target, load_sem.at[i, 0])
+        for i, (source, target) in enumerate(
+            [(pbl_hbm, pbl), (strength_hbm, strength), (level_hbm, level)]
+        )
     ]
-    for copy in aux:
+    for copy in aux[len(blocks):]:
         copy.start()
 
     def tiles_of(j):
@@ -266,6 +267,8 @@
     ready = 0
     for b in range(len(blocks)):
         along_rows(b)
+        if b < len(aux):
+            aux[b].start()
         if ready < last and blocks[b][0] >= sum(groups[ready][:2]):
             along_cols(ready)
             send(ready)
@@ -314,8 +317,9 @@
         first, count, fold, tile = groups[j]
         span = slice(tile * SUB, tile * SUB + KX // fold)
         hi, lo = expand_cols([(coef_ref[span] * scale_ref[span], count, fold)], col_ref[...])
-        wave[j % 2, 0, :count * KX] = hi
-        wave[j % 2, 1, :count * KX] = lo
+        keep = wide_ref if j == early - 1 else wave.at[j % 2]
+        keep[0, :count * KX] = hi
+        keep[1, :count * KX] = lo
 
     def finish(j):
         first, count, fold, tile = groups[j]
@@ -342,8 +346,6 @@
         widen(j)
         if j:
             finish(j - 1)
-    if early:
-        finish(early - 1)
     arrive(early)
     settle_tiles(mine, part_send, 0, tiles, sum(owns), n_owned)
     for c in range(1, n_owned + 1):
@@ -351,13 +353,14 @@
 
 
 def synthesis_kernel(
-    tail, coef_ref, scale_ref, weight_ref, row_ref, col_ref, early_ref, tend_hbm, energy_hbm,
+    tail, coef_ref, scale_ref, weight_ref, row_ref, col_ref, early_ref, wide_ref,
+    tend_hbm, energy_hbm,
     tend, energy_ref, tend_sem, energy_sem,
 ):
     levels, variables = energy_ref.shape
     fields = levels * variables
     groups, tiles = plan_groups(fields)
-    done = groups[-tail][0]
+    done, wide = groups[-tail - 1][:2]
 
     def out(first, count):
         level, at = first // variables, first % variables
@@ -394,10 +397,10 @@
         parts.append((coef_ref[span] * scale_ref[span], count, fold))
     hi, lo = expand_cols(parts, col_ref[...])
     for f in range(done, fields):
-        span = slice((f - done) * KX, (f - done + 1) * KX)
-        tend[f - done] = expand_rows(
-            hi[span], lo[span], row_ref[...], weight_ref[f // variables]
-        )
+        k = f - done if f < done + wide else f - done - wide
+        span = slice(k * KX, (k + 1) * KX)
+        pair = (wide_ref[0, span], wide_ref[1, span]) if f < done + wide else (hi[span], lo[span])
+        tend[f - done] = expand_rows(*pair, row_ref[...], weight_ref[f // variables])
         if f > done:
             out(f - 1, 1).start()
     out(fields - 1, 1).start()
@@ -412,9 +415,9 @@
     n_dev = gx * gy
     groups, tiles = plan_groups(fields)
     n_owned = max(plan_owners(gx, gy, tiles)[1]) + 1
-    tail = min(TAIL, len(groups))
+    tail = min(TAIL, len(groups) - 1)
     blocks = plan_blocks(fields)
-    done = groups[-tail][0]
+    done = groups[-tail - 1][0]
     anywhere = pl.BlockSpec(memory_space=pl.ANY)
     vmem = pl.BlockSpec(memory_space=pltpu.VMEM)
     dma = pltpu.SemaphoreType.DMA
@@ -427,9 +430,10 @@
             pltpu.VMEM((rows, 4 * KX), BF16),
             pltpu.VMEM((3 * LANES, cols), BF16),
             pltpu.VMEM((max(done, 1), rows, cols), BF16),
+            pltpu.VMEM((2, LANES, cols), BF16),
         ),
         in_specs=[anywhere] * 5,
-        out_specs=(vmem,) * 6,
+        out_specs=(vmem,) * 7,
         scratch_shapes=[
             pltpu.SMEM((levels, variables), F32),
             pltpu.SMEM((levels,), F32),
@@ -441,8 +445,7 @@
             pltpu.VMEM((n_owned, n_dev - 1, SUB, LANES), F32),
             pltpu.VMEM((tiles, SUB, LANES), F32),
             pltpu.VMEM((2, 2, LANES, cols), BF16),
-            dma((len(blocks), 1 + max(len(b) % 2 for b in blocks))),
-            dma((3,)),
+            dma((max(len(blocks), 3), 1 + max(len(b) % 2 for b in blocks))),
             dma,
             dma((n_owned,)),
             dma,
@@ -463,7 +466,7 @@
             jax.ShapeDtypeStruct((levels, variables, rows, cols), BF16),
             jax.ShapeDtypeStruct((levels, variables), F32),
         ),
-        in_specs=[vmem] * 6,
+        in_specs=[vmem] * 7,
         out_specs=(anywhere, anywhere),
         scratch_shapes=[
             pltpu.VMEM((fields - done, rows, cols), BF16),

time: 16.4 us -> 16.2 us (0.988)
  Pallas kernels: 15.6 us -> 15.4 us
    pallas_call x1, Pallas kernels: 14.1 us -> 14 us  [per_device(): pl.pallas_call(functools.partial(analysis_kernel, (gx, gy, tail)), out_sh...]
where the time goes in v5:
time: 16.2 us; the launch traced here: 16 us
  Pallas kernels  15.4 us (95%)
  between operations  0.64 us (4%)
    pallas_call x1, Pallas kernels, per_device(): pl.pallas_call(functools.partial(analysis_kernel, (gx, gy, tail)), out_sh...  14 us
    pallas_call x1, Pallas kernels, per_device(): pl.pallas_call(functools.partial(synthesis_kernel, tail), out_shape=(jax....  1.42 us

profile of v5, /device:TPU:0, one launch (start us, length us, event | category | flops | bytes accessed | tf_op | source)
XLA Modules:
  0.0 16.0 jit_solution(97877387904502263)
XLA Ops:
  0.6 14.0 %analysis.1 = (f32[144,128]{1,0:T(8,128)S(1)}, f32[144,128]{1,0:T(8,128)S(1)}, f32[3,128,512]{2,1,0:T(8,128)S(1)}, bf16[128,128]{1,0:T(8,128)(2,1)S(1)}, bf16[38...) custom-call(f32[18,128,512]{2,1,0:T(8,128)} %bitcast.2, ...), custom_call_target="tpu_custom_call" | custom-call | tf_op jit(solution)/shard_map/analysis/pallas_call | solution.py:424
  14.6 1.4 %synthesis.1 = (bf16[3,6,128,512]{3,2,1,0:T(8,128)(2,1)}, f32[3,6]{1,0:T(4,128)}) custom-call(f32[144,128]{1,0:T(8,128)S(1)} %get-tuple-element.9.coef_ref, f32[144,128]{1,0:T(8,128)S(1)} %get-tuple-element.10.scale_ref, f32[3,128,512]{2,1,0:T(8,128)S(1)} %get-tuple-element.11.weight_ref, bf16[128,128]{1,0:T(8,128)(2,1)S(1)} %get-tuple-element.12.row_ref, ...), custom_call_target="tpu_custom_call" | custom-call | tf_op jit(solution)/shard_map/synthesis/pallas_call | solution.py:463

commit v6 on v5

--- a/solution.py
+++ b/solution.py
@@ -15,7 +15,7 @@
 SUB = 8
 MESH = pl.DeviceIdType.MESH
 REACH = 3
-FAR = 3
+EARLY = 4
 TAIL = 2
 BLOCK = 4
 
@@ -73,6 +73,20 @@
     owners = [near[t % len(near)] for t in range(tiles)]
     places = [owners[:t].count(owners[t]) for t in range(tiles)]
     return owners, places
+
+
+def plan_gates(gx, gy, owners, last):
+    def spot(p):
+        return p[0] // 4, (p[0] // 2) % 2, p[1]
+
+    def wait(p):
+        apart = [sum(abs(a - b) for a, b in zip(spot(p), spot(o))) for o in owners]
+        return max(hops(*o) + d for o, d in zip(owners, apart)) - hops(*p)
+
+    every = [(ix, iy) for ix in range(gx) for iy in range(gy)]
+    return [
+        (p, min(max(wait(p) - EARLY, 0), last) if hops(*p) else last) for p in every
+    ]
 
 
 def lane_group(rows):
@@ -116,7 +130,10 @@
     n_owned = max(places) + 1
     ix, iy = lax.axis_index("gx"), lax.axis_index("gy")
     me = ix * gy + iy
-    far = hops(ix, iy)
+
+    def at(p):
+        return (ix == p[0]) & (iy == p[1])
+
 
     def settle(ref, sem):
         pltpu.make_async_copy(ref, ref, sem).wait()
@@ -156,7 +173,7 @@
         return range(tile, tile + KX // fold // SUB)
 
     def owned(t):
-        return (ix == owners[t][0]) & (iy == owners[t][1])
+        return at(owners[t])
 
     def count_owned(k, weigh):
         return sum(
@@ -250,7 +267,10 @@
             mine[t] = coef[k * SUB:(k + 1) * SUB]
 
     last = len(groups) - 1
-    gate = jnp.where(far >= FAR, 0, jnp.where(far > 0, max(last - 1, 0), last))
+    gate = sum(
+        (at(p).astype(jnp.int32) * g for p, g in plan_gates(gx, gy, owners, last) if g),
+        jnp.int32(0),
+    )
 
     def send(j):
         @pl.when(gate == j)

time: 16.2 us -> 16.1 us (level)
  no operation moved by 1% of the time
where the time goes in v6:
time: 16.1 us; the launch traced here: 15.9 us
  Pallas kernels  15.3 us (95%)
  between operations  0.64 us (4%)
    pallas_call x1, Pallas kernels, per_device(): pl.pallas_call(functools.partial(analysis_kernel, (gx, gy, tail)), out_sh...  13.9 us
    pallas_call x1, Pallas kernels, per_device(): pl.pallas_call(functools.partial(synthesis_kernel, tail), out_shape=(jax....  1.42 us

profile of v6, /device:TPU:0, one launch (start us, length us, event | category | flops | bytes accessed | tf_op | source)
XLA Modules:
  0.0 15.9 jit_solution(5622164069881860260)
XLA Ops:
  0.6 13.9 %analysis.1 = (f32[144,128]{1,0:T(8,128)S(1)}, f32[144,128]{1,0:T(8,128)S(1)}, f32[3,128,512]{2,1,0:T(8,128)S(1)}, bf16[128,128]{1,0:T(8,128)(2,1)S(1)}, bf16[38...) custom-call(f32[18,128,512]{2,1,0:T(8,128)} %bitcast.2, ...), custom_call_target="tpu_custom_call" | custom-call | tf_op jit(solution)/shard_map/analysis/pallas_call | solution.py:444
  14.5 1.4 %synthesis.1 = (bf16[3,6,128,512]{3,2,1,0:T(8,128)(2,1)}, f32[3,6]{1,0:T(4,128)}) custom-call(f32[144,128]{1,0:T(8,128)S(1)} %get-tuple-element.9.coef_ref, f32[144,128]{1,0:T(8,128)S(1)} %get-tuple-element.10.scale_ref, f32[3,128,512]{2,1,0:T(8,128)S(1)} %get-tuple-element.11.weight_ref, bf16[128,128]{1,0:T(8,128)(2,1)S(1)} %get-tuple-element.12.row_ref, ...), custom_call_target="tpu_custom_call" | custom-call | tf_op jit(solution)/shard_map/synthesis/pallas_call | solution.py:483

commit v7 on v6

--- a/solution.py
+++ b/solution.py
@@ -87,6 +87,17 @@
     return [
         (p, min(max(wait(p) - EARLY, 0), last) if hops(*p) else last) for p in every
     ]
+
+
+def add_tiles(got, k):
+    count = got.shape[1]
+    if count > 64:
+        return jnp.sum(got[k], axis=0)
+    terms = [got[k, i] for i in range(count)]
+    while len(terms) > 1:
+        odd = terms[len(terms) & ~1:]
+        terms = [x + y for x, y in zip(terms[::2], terms[1::2])] + odd
+    return terms[0]
 
 
 def lane_group(rows):
@@ -330,7 +341,7 @@
         def _(k=k):
             t = tile_at[k]
             settle(got.at[k], part_recv.at[k])
-            full[t] = mine[t] + jnp.sum(got[k], axis=0)
+            full[t] = mine[t] + add_tiles(got, k)
             each_other(lambda target: to_all(t, group_at[k], target).start())
 
     def widen(j):

time: 16.1 us -> 16.1 us (level)
  no operation moved by 1% of the time
where the time goes in v7:
time: 16.1 us; the launch traced here: 15.9 us
  Pallas kernels  15.3 us (95%)
  between operations  0.64 us (4%)
    pallas_call x1, Pallas kernels, per_device(): pl.pallas_call(functools.partial(analysis_kernel, (gx, gy, tail)), out_sh...  13.9 us
    pallas_call x1, Pallas kernels, per_device(): pl.pallas_call(functools.partial(synthesis_kernel, tail), out_shape=(jax....  1.42 us

profile of v7, /device:TPU:0, one launch (start us, length us, event | category | flops | bytes accessed | tf_op | source)
XLA Modules:
  0.0 15.9 jit_solution(5410335576166579753)
XLA Ops:
  0.6 13.9 %analysis.1 = (f32[144,128]{1,0:T(8,128)S(1)}, f32[144,128]{1,0:T(8,128)S(1)}, f32[3,128,512]{2,1,0:T(8,128)S(1)}, bf16[128,128]{1,0:T(8,128)(2,1)S(1)}, bf16[38...) custom-call(f32[18,128,512]{2,1,0:T(8,128)} %bitcast.2, ...), custom_call_target="tpu_custom_call" | custom-call | tf_op jit(solution)/shard_map/analysis/pallas_call | solution.py:455
  14.5 1.4 %synthesis.1 = (bf16[3,6,128,512]{3,2,1,0:T(8,128)(2,1)}, f32[3,6]{1,0:T(4,128)}) custom-call(f32[144,128]{1,0:T(8,128)S(1)} %get-tuple-element.9.coef_ref, f32[144,128]{1,0:T(8,128)S(1)} %get-tuple-element.10.scale_ref, f32[3,128,512]{2,1,0:T(8,128)S(1)} %get-tuple-element.11.weight_ref, bf16[128,128]{1,0:T(8,128)(2,1)S(1)} %get-tuple-element.12.row_ref, ...), custom_call_target="tpu_custom_call" | custom-call | tf_op jit(solution)/shard_map/synthesis/pallas_call | solution.py:494
